TPU v7x, 256 devices: a whole 4x4x8 slice. The times are simulated.
256 devices in a mesh: dp: 64 (over x, z, core), mp: 4 (over y).
Axes of the slice: x: 4, y: 4, z: 8, core: 2. Of those that a mesh axis runs over, the one named last changes fastest.
Arguments:
- features: bfloat16 [16384, 512], P('dp'), may hold values from -6 to 6
- adjacency: bfloat16 [4096, 4, 128, 128], P('dp'), may hold values from -0.125 to 0.125
- source_block: int32 [4096, 4], P('dp'), may hold values from 0 to 1
- edge_type: int32 [4096, 4], P('dp'), may hold values from 0 to 19
- target_block: int32 [4096, 4], P('dp'), may hold values from 0 to 1
- live_count: int32 [64, 64], P('dp'), may hold values from 3 to 4, as said below
- relation_weight: bfloat16 [20, 512, 512], P(None, None, 'mp'), may hold values from -0.25 to 0.25
- self_weight: bfloat16 [512, 512], P(None, 'mp'), may hold values from -0.25 to 0.25
- layer_bias: bfloat16 [512], P('mp'), may hold values from -3 to 3
- norm_gain: bfloat16 [512], replicated, may hold values from 0.5 to 1.5
Outputs:
- node_states: bfloat16 [16384, 512], P(('dp', 'mp'))
Inputs may be any that keep to these rules, and one draw needn't show every extreme that they name: `source_block`: row s * 64 + d names a block among sender s's 2 blocks. `target_block`: row d * 64 + s names a block among receiver d's 2 blocks. live_count[d, s] live slots from sender s to receiver d, the first ones; some receiver has all 4 slots live from every sender.
All inputs are finite; a program needn't handle non-finite values.
Results may differ from a plain program's by a relative error of at most 0.007.
Values may be sent and summed in bfloat16 or wider, within the bound.
A program may use at most 128 MiB of HBM per device.

v0:
```python
import jax
import jax.numpy as jnp
from jax import lax
from jax.sharding import PartitionSpec as P

BLK = 128


epsilon = 1e-05


def sent_together(arrays, axis, split_dim, concat_dim, along):
    widths = [a.shape[along] for a in arrays]
    both = jnp.concatenate(arrays, axis=along)
    filled = lax.all_to_all(both, axis, split_axis=split_dim, concat_axis=concat_dim, tiled=True)
    return tuple(jnp.split(filled, [sum(widths[:k]) for k in range(1, len(widths))], axis=along))


def split_up(shard, dim, peers):
    dims = shard.shape
    tiles = shard.reshape(*dims[:dim], peers, dims[dim] // peers, *dims[dim + 1 :])
    return jnp.moveaxis(tiles, dim, 0)


def summed_on_arrival(shard, axis, dim):
    peers = lax.axis_size(axis)
    tiles = lax.all_to_all(split_up(shard, dim, peers), axis, 0, 0, tiled=True)
    return jnp.sum(tiles.astype(jnp.float32), axis=0)


def block_table(features, relation_weight, blocks):
    stacked = features.reshape(blocks, BLK, features.shape[1])
    lookup = jnp.einsum(
        "bid,rdc->bric", stacked, relation_weight, preferred_element_type=jnp.float32
    )
    return lookup.astype(jnp.bfloat16).reshape(
        blocks * relation_weight.shape[0], BLK, relation_weight.shape[2]
    )


def transform_slots(lookup, lookup_rows, adj_tiles):
    chosen = jnp.take(lookup, lookup_rows, axis=0)
    return jnp.einsum("nij,njc->nic", adj_tiles, chosen, preferred_element_type=jnp.float32)


def selector(targets, counts, blocks):
    slot_count = targets.shape[1]
    active = jnp.arange(slot_count, dtype=jnp.int32)[None, :] < counts[:, None]
    matches = targets[:, :, None] == jnp.arange(blocks, dtype=jnp.int32)[None, None, :]
    return jnp.logical_and(matches, active[:, :, None]).astype(jnp.float32)


def per_device(
    features,
    adjacency,
    source_block,
    edge_type,
    target_block,
    live_count,
    relation_weight,
    self_weight,
    layer_bias,
    norm_gain,
):
    peer_count = lax.axis_size("dp")
    slot_count = source_block.shape[1]
    node_rows = features.shape[0]
    blocks = node_rows // BLK
    columns = relation_weight.shape[2]
    lookup = block_table(features, relation_weight, blocks)
    lookup_rows = (source_block * relation_weight.shape[0] + edge_type).reshape(
        peer_count * slot_count
    )
    flat_tiles = adjacency.reshape(peer_count * slot_count, BLK, BLK)
    routed, routed_count = sent_together(
        (target_block, live_count.reshape(peer_count, 1)), "dp", 0, 0, 1
    )
    weights = selector(routed, routed_count[:, 0], blocks)
    receivers = node_rows * lax.axis_size("dp") // node_rows
    message = transform_slots(lookup, lookup_rows, flat_tiles).reshape(
        receivers, slot_count, BLK * columns
    )
    summed = jnp.einsum("rkb,rkx->rbx", weights, message, precision=lax.Precision.HIGHEST)
    aggregate = summed_on_arrival(
        summed.reshape(receivers * blocks * BLK, columns).astype(jnp.bfloat16), "dp", 0
    )
    own_term = jnp.dot(features, self_weight, preferred_element_type=jnp.float32)
    hidden = jax.nn.relu(own_term + aggregate + layer_bias.astype(jnp.float32)).astype(jnp.bfloat16)
    by_rows = lax.all_to_all(hidden, "mp", split_axis=0, concat_axis=1, tiled=True)
    values = by_rows.astype(jnp.float32)
    inverse_rms = lax.rsqrt(jnp.mean(values * values, axis=1, keepdims=True) + epsilon)
    return (values * inverse_rms * norm_gain.astype(jnp.float32)).astype(jnp.bfloat16)


def solution(mesh):
    return jax.shard_map(
        per_device,
        mesh=mesh,
        in_specs=(
            P("dp", None),
            P("dp", None, None, None),
            P("dp", None),
            P("dp", None),
            P("dp", None),
            P("dp", None),
            P(None, None, "mp"),
            P(None, "mp"),
            P("mp"),
            P(),
        ),
        out_specs=P(("dp", "mp"), None),
        check_vma=False,
    )
```

profile of v0, /device:TPU:1, one launch (start us, length us, event | category | flops | bytes accessed | tf_op | source)
XLA Modules:
  0.0 229.2 jit_solution(922433717765947294)
XLA Ops:
  0.0 0.0 copy-start
  0.0 0.9 pad_add_fusion
  0.9 0.7 copy.40
  1.6 13.0 %all-to-all-start = ((s32[64,1,5]{2,1,0:T(1,128)}), s32[64,1,5]{2,1,0:T(1,128)S(1)}, u32[]{:S(2)}, u32[]{:S(2)}) async-start(s32[64,1,5]{2,1,0:T(1,128)} %bitcast.1), calls=%async_computation | async-start | bytes 65536 | tf_op jit(solution)/shard_map/all_to_all | solution.py:15
  14.6 0.7 multiply_add_fusion
  15.3 0.1 copy.41
  15.4 0.1 reshape.102
  15.5 0.1 reshape.99
  15.6 0.0 copy-done
  15.6 2.9 %fusion.8 = bf16[2,20,128,128]{2,3,0,1:T(8,128)(2,1)} fusion(bf16[2,128,512,1]{2,1,0,3:T(8,128)(2,1)} %bitcast.41, bf16[20,512,128]{2,1,0:T(8,128)(2,1)S(1)} %copy-done), kind=kOutput, calls=%fused_computation.10 | convolution fusion | flops 671744000 | bytes 4194304 | tf_op jit(solution)/shard_map/bid,rdc->bric/dot_general | solution.py:33
  18.5 1.8 copy.43
  20.3 8.6 %gather_fusion = bf16[256,128,128]{2,1,0:T(8,128)(2,1)} fusion(bf16[40,128,128]{2,1,0:T(8,128)(2,1)S(1)} %bitcast.39, s32[1024]{0:T(1024)S(1)} %pad_clamp_fusion), kind=kCustom, calls=%fused_computation | custom fusion | bytes 16778240 | tf_op jit(solution)/shard_map/jit(_take)/gather | solution.py:42
  28.9 13.2 %convolution_bitcast_fusion = f32[256,128,128]{1,2,0:T(8,128)} fusion(bf16[256,128,128]{2,1,0:T(8,128)(2,1)} %bitcast.40, bf16[256,128,128]{2,1,0:T(8,128)(2,1)} %gather_fusion, pred[256]{0:T(512)(128)(4,1)S(1)} %compare_and_fusion), kind=kOutput, calls=%fused_computation.2 | convolution fusion | flops 1077936128 | bytes 33554688 | tf_op jit(solution)/shard_map/nij,njc->nic/dot_general | solution.py:43
  42.1 17.5 %copy.46 = f32[256,128,128]{2,1,0:T(8,128)} copy(f32[256,128,128]{1,2,0:T(8,128)} %convolution_bitcast_fusion) | data formatting | bytes 33554432 | tf_op jit(solution)/shard_map/nij,njc->nic/dot_general | solution.py:43
  59.6 20.2 %reshape.104 = f32[64,4,16384]{2,1,0:T(4,128)} reshape(f32[256,128,128]{2,1,0:T(8,128)} %copy.46) | data formatting | bytes 33554432 | tf_op jit(solution)/shard_map/reshape | solution.py:80
  79.8 0.0 all-to-all-done
  79.8 0.2 slice_reduce_fusion
  80.0 0.1 iota_compare_fusion
  80.1 21.4 %convolution_convert_fusion = bf16[64,2,16384]{2,1,0:T(2,128)(2,1)} fusion(f32[64,4,16384]{2,1,0:T(4,128)} %reshape.104, pred[64,4]{1,0:T(8,128)(4,1)S(1)} %iota_compare_fusion, s32[64,4]{1,0:T(8,128)S(1)} %bitcast.43), kind=kOutput, calls=%fused_computation.1 | convolution fusion | flops 102761472 | bytes 20972800 | tf_op jit(solution)/shard_map/rkb,rkx->rbx/dot_general | solution.py:83
  101.5 8.0 %convert_element_type.45 = bf16[64,256,128]{2,1,0:T(8,128)(2,1)} reshape(bf16[64,2,16384]{2,1,0:T(2,128)(2,1)} %convolution_convert_fusion) | data formatting | bytes 8388608 | tf_op jit(solution)/shard_map/convert_element_type | solution.py:85
  109.5 10.7 %all-to-all-start.1 = ((bf16[64,256,128]{2,1,0:T(8,128)(2,1)}), bf16[64,256,128]{2,1,0:T(8,128)(2,1)}, u32[]{:S(2)}, u32[]{:S(2)}) async-start(bf16[64,256,128]{2,1,0:T(8,128)(2,1)} %convert_element_type.45), calls=%async_computation.1 | async-start | bytes 8388608 | tf_op jit(solution)/shard_map/all_to_all | solution.py:27
  120.1 0.0 copy-done.5
  120.2 95.8 %all-to-all-done.1 = bf16[64,256,128]{2,1,0:T(8,128)(2,1)} async-done(((bf16[64,256,128]{2,1,0:T(8,128)(2,1)}), bf16[64,256,128]{2,1,0:T(8,128)(2,1)}, u32[]{:S(2)}, u32[]{:S(2)}) %all-to-all-start.1) | async-done | bytes 4194336 | tf_op jit(solution)/shard_map/all_to_all | solution.py:27
  216.0 2.8 %convert_reduce_fusion = f32[256,128]{1,0:T(8,128)S(1)} fusion(bf16[64,256,128]{2,1,0:T(8,128)(2,1)} %all-to-all-done.1), kind=kLoop, calls=%fused_computation.3 | loop fusion | flops 4161536 | bytes 4325376 | tf_op jit(solution)/shard_map/reduce_sum | solution.py:28
  218.8 0.0 copy-done.2
  218.8 0.0 copy-done.3
  218.8 0.9 fusion.13
  219.7 4.2 %all-to-all-start.2 = ((bf16[4,64,128]{2,1,0:T(8,128)(2,1)}), bf16[4,64,128]{2,1,0:T(8,128)(2,1)S(1)}, u32[]{:S(2)}, u32[]{:S(2)}) async-start(bf16[4,64,128]{2,1,0:T(8,128)(2,1)} %bitcast.11), calls=%async_computation.2 | async-start | bytes 131072 | tf_op jit(solution)/shard_map/all_to_all | solution.py:89
  223.8 0.0 copy-done.4
  223.8 4.5 %all-to-all-done.2 = bf16[4,64,128]{2,1,0:T(8,128)(2,1)S(1)} async-done(((bf16[4,64,128]{2,1,0:T(8,128)(2,1)}), bf16[4,64,128]{2,1,0:T(8,128)(2,1)S(1)}, u32[]{:S(2)}, u32[]{:S(2)}) %all-to-all-start.2) | async-done | bytes 65568 | tf_op jit(solution)/shard_map/all_to_all | solution.py:89
  228.3 0.1 fusion.14
  228.4 0.7 fusion.16
  (12 shorter events, 0.0 us)
Async XLA Ops:
  0.0 15.6 %copy-start = (bf16[20,512,128]{2,1,0:T(8,128)(2,1)S(1)}, bf16[20,512,128]{2,1,0:T(8,128)(2,1)}, u32[]{:S(2)}) copy-start(bf16[20,512,128]{2,1,0:T(8,128)(2,1)} %param.16) | copy-start | bytes 7864324
  1.6 78.2 %all-to-all-start = ((s32[64,1,5]{2,1,0:T(1,128)}), s32[64,1,5]{2,1,0:T(1,128)S(1)}, u32[]{:S(2)}, u32[]{:S(2)}) async-start(s32[64,1,5]{2,1,0:T(1,128)} %bitcast.1), calls=%async_computation | async-start | bytes 65536 | tf_op jit(solution)/shard_map/all_to_all | solution.py:15
  101.5 18.6 %copy-start.5 = (bf16[128]{0:T(256)(128)(2,1)S(1)}, bf16[128]{0:T(256)(128)(2,1)}, u32[]{:S(2)}) copy-start(bf16[128]{0:T(256)(128)(2,1)} %param.18) | copy-start | bytes 772
  101.5 127.7 %copy-start.1 = (bf16[20,512,128]{2,1,0:T(8,128)(2,1)S(1)}, bf16[20,512,128]{2,1,0:T(8,128)(2,1)}, u32[]{:S(2)}) copy-start(bf16[20,512,128]{2,1,0:T(8,128)(2,1)} %param.16) | copy-start | bytes 7864324
  109.5 109.3 %copy-start.2 = (bf16[256,512]{1,0:T(8,128)(2,1)S(1)}, bf16[256,512]{1,0:T(8,128)(2,1)}, u32[]{:S(2)}) copy-start(bf16[256,512]{1,0:T(8,128)(2,1)} %param.10) | copy-start | bytes 786436
  109.5 109.3 %copy-start.3 = (bf16[512,128]{1,0:T(8,128)(2,1)S(1)}, bf16[512,128]{1,0:T(8,128)(2,1)}, u32[]{:S(2)}) copy-start(bf16[512,128]{1,0:T(8,128)(2,1)} %param.17) | copy-start | bytes 393220
  109.5 114.4 %copy-start.4 = (bf16[512]{0:T(512)(128)(2,1)S(1)}, bf16[512]{0:T(512)(128)(2,1)}, u32[]{:S(2)}) copy-start(bf16[512]{0:T(512)(128)(2,1)} %param.19) | copy-start | bytes 3076
  109.5 106.5 %all-to-all-start.1 = ((bf16[64,256,128]{2,1,0:T(8,128)(2,1)}), bf16[64,256,128]{2,1,0:T(8,128)(2,1)}, u32[]{:S(2)}, u32[]{:S(2)}) async-start(bf16[64,256,128]{2,1,0:T(8,128)(2,1)} %convert_element_type.45), calls=%async_computation.1 | async-start | bytes 8388608 | tf_op jit(solution)/shard_map/all_to_all | solution.py:27
  219.7 8.7 %all-to-all-start.2 = ((bf16[4,64,128]{2,1,0:T(8,128)(2,1)}), bf16[4,64,128]{2,1,0:T(8,128)(2,1)S(1)}, u32[]{:S(2)}, u32[]{:S(2)}) async-start(bf16[4,64,128]{2,1,0:T(8,128)(2,1)} %bitcast.11), calls=%async_computation.2 | async-start | bytes 131072 | tf_op jit(solution)/shard_map/all_to_all | solution.py:89
where the time goes:
time: 230 us; the launch traced here: 229 us
  waiting for transfers between devices  100 us (43%)
  local copies, waits for them, and re-layouts  57.3 us (25%)
  matrix products  38.4 us (17%)
  starting transfers between devices  27.8 us (12%)
  other arithmetic  5.3 us (2%)
    all_to_all x1, waiting for transfers between devices, summed_on_arrival(): tiles = lax.all_to_all(split_up(shard, dim, peers), axis, 0, 0, tiled=True)  95.8 us
    dot_general x1, matrix products, per_device(): jnp.einsum('rkb,rkx->rbx', weights, message, precision=lax.Precision.HIGH...  21.4 us
    reshape x1, local copies, waits for them, and re-layouts, per_device(): transform_slots(lookup, lookup_rows, flat_tiles)  20.2 us
    dot_general x1, local copies, waits for them, and re-layouts, transform_slots(): jnp.einsum('nij,njc->nic', adj_tiles, chosen, preferred_element_type=jnp....  17.5 us
    dot_general x1, matrix products, transform_slots(): jnp.einsum('nij,njc->nic', adj_tiles, chosen, preferred_element_type=jnp....  13.2 us
    all_to_all x1, starting transfers between devices, sent_together(): lax.all_to_all(both, axis, split_axis=split_dim, concat_axis=concat_dim,...  13 us
    all_to_all x1, starting transfers between devices, summed_on_arrival(): tiles = lax.all_to_all(split_up(shard, dim, peers), axis, 0, 0, tiled=True)  10.7 us
    gather x1, local copies, waits for them, and re-layouts, transform_slots(): chosen = jnp.take(lookup, lookup_rows, axis=0)  8.61 us
  transfers between devices with their start and end apart: 3, of which 2 were waited for; matrix products, arithmetic and copies ran while one was open for 28% of the time, Pallas kernels for 0%

commit v1 on v0

v1 whole, which is shorter than its diff:
```python
import functools

import jax
import jax.numpy as jnp
from jax import lax
from jax.experimental import pallas as pl
from jax.experimental.pallas import tpu as pltpu
from jax.sharding import PartitionSpec as P

BLK = 128
NX, NZ, NY = 4, 8, 4
GROUP = 2 * NX
PEERS = NX * NZ * 2
SLOTS = 4
BLOCKS = 2
ADJ_CHUNKS = 8
EPSILON = 1e-05
MESH = pl.DeviceIdType.MESH

X_FAR_PLUS = (4, 3, 2, 1)
Z_FAR_PLUS = (1,)
ROW_ORDER = (4, 3, 5, 2, 6, 1, 7, 0)


def pieces():
    table = {}
    for dz in range(NZ):
        plus = dz in X_FAR_PLUS
        far = ("xf", dz)
        table[far] = (2, dz, 0, (), "x+" if plus else "x-")
        table[("xp", dz)] = (1, dz, 0, (far,) if plus else (), "x+")
        table[("xm", dz)] = (3, dz, 0, () if plus else (far,), "x-")
    for dz, before, way in (
        (4, None, "z+"), (3, 4, "z+"), (2, 3, "z+"), (1, 2, "z+"), (5, None, "z-"), (6, 5, "z-"), (7, 6, "z-"),
    ):
        chain = () if before is None else (("az", before),)
        table[("az", dz)] = (0, dz, 0, (("xp", dz), ("xm", dz)) + chain, way)
    table[("fa",)] = (0, 0, 0, (("xp", 0), ("xm", 0), ("az", 1), ("az", 7)), None)
    for dx in range(NX):
        plus = dx in Z_FAR_PLUS
        far = ("bz", 4, dx)
        table[far] = (dx, 4, 1, (), "z+" if plus else "z-")
        table[("bz", 3, dx)] = (dx, 3, 1, (far,) if plus else (), "z+")
        table[("bz", 5, dx)] = (dx, 5, 1, () if plus else (far,), "z-")
        for dz, before, way in ((2, 3, "z+"), (1, 2, "z+"), (6, 5, "z-"), (7, 6, "z-")):
            table[("bz", dz, dx)] = (dx, dz, 1, (("bz", before, dx),), way)
    for dx, before, way in ((2, None, "x+"), (1, 2, "x+"), (3, None, "x-")):
        chain = () if before is None else (("bx", before),)
        table[("bx", dx)] = (dx, 0, 1, (("bz", 1, dx), ("bz", 7, dx)) + chain, way)
    table[("fb",)] = (0, 0, 1, (("bz", 1, 0), ("bz", 7, 0), ("bx", 1), ("bx", 3)), None)
    return table


ORDER = (
    ("bz", 4, 2), ("xf", 4), ("xm", 4), ("bz", 4, 1), ("bz", 4, 3), ("bz", 4, 0), ("xf", 3), ("bz", 3, 2),
    ("xm", 3), ("bz", 3, 3), ("bz", 3, 0), ("xf", 5), ("xp", 5), ("bz", 5, 1), ("xf", 2), ("xm", 2),
    ("xf", 6), ("xp", 6), ("xf", 1), ("xm", 1), ("xf", 7), ("xp", 7), ("xf", 0), ("xp", 0), ("bz", 5, 2),
    ("xp", 4), ("bz", 3, 1), ("bz", 5, 3), ("xp", 3), ("bz", 2, 2), ("bz", 5, 0), ("xm", 5), ("bz", 2, 3),
    ("bz", 6, 1), ("xp", 2), ("bz", 2, 0), ("xm", 6), ("bz", 6, 2), ("bz", 2, 1), ("xp", 1), ("bz", 6, 3),
    ("bz", 1, 2), ("xm", 7), ("bz", 6, 0), ("bz", 1, 3), ("xm", 0), ("bz", 7, 1), ("bz", 1, 0), ("az", 4),
    ("az", 5), ("bz", 7, 2), ("bz", 1, 1), ("bz", 7, 3), ("bz", 7, 0), ("az", 6), ("az", 3), ("bx", 2),
    ("bx", 3), ("az", 7), ("az", 2), ("bx", 1), ("az", 1), ("fb",), ("fa",),
)
PIECES = pieces()
SENT = tuple(name for name in PIECES if PIECES[name][4] is not None)
SLOT_OF = {name: n for n, name in enumerate(SENT)}


def layer_kernel(
    feat_in, adj_in, source_in, type_in, target_in, live_in, rel_in, self_in, bias_in, gain_in, out_ref,
    feat, adj, target, live, rel, self_w, bias, gain,
    table, msg, codes, by_group, group_got, by_z, z_got, weight,
    base, core_send, core_got, send_buf, got_buf, hidden, gathered,
    load_sem, adj_sem, send1, recv1, send2, recv2, core_s, core_r, piece_s, piece_r, mp_s, mp_r,
):
    me = lax.axis_index("dp")
    y = lax.axis_index("mp")
    c = me % 2
    z = (me // 2) % NZ
    x = me // (2 * NZ)
    p = x * 2 + c
    f32 = jnp.float32

    def dp_index(xi, zi, ci):
        return (xi * NZ + zi) * 2 + ci

    def at(dp, mp=None):
        return {"dp": dp, "mp": y if mp is None else mp}

    loads = [
        pltpu.make_async_copy(src, dst, load_sem.at[n])
        for n, (src, dst) in enumerate(
            ((target_in, target), (live_in, live), (feat_in, feat), (rel_in, rel),
             (self_in, self_w), (bias_in, bias), (gain_in, gain))
        )
    ]
    for load in loads[:4]:
        load.start()

    def adj_load(chunk):
        per = PEERS * SLOTS // ADJ_CHUNKS
        rows = pl.ds(chunk * per, per)
        return pltpu.make_async_copy(adj_in.at[rows], adj.at[rows], adj_sem.at[chunk])

    for chunk in range(ADJ_CHUNKS):
        adj_load(chunk).start()
    for load in loads[4:]:
        load.start()

    barrier = pltpu.get_barrier_semaphore()
    for j in range(1, GROUP):
        q = (p + j) % GROUP
        pl.semaphore_signal(barrier, inc=1, device_id=at(dp_index(q // 2, z, q % 2)), device_id_type=MESH)
    for j in range(1, NZ):
        pl.semaphore_signal(barrier, inc=1, device_id=at(dp_index(x, (z + j) % NZ, c)), device_id_type=MESH)
    for j in range(1, NY):
        pl.semaphore_signal(barrier, inc=1, device_id=at(me, (y + j) % NY), device_id_type=MESH)

    loads[0].wait()
    loads[1].wait()
    slot = lax.broadcasted_iota(jnp.int32, (SLOTS, PEERS), 0)
    codes[...] = jnp.zeros_like(codes)
    codes[0:SLOTS, 0:PEERS] = jnp.where(slot < live[...], target[...], BLOCKS)
    codes[...] = jnp.transpose(codes[...])
    for q in range(GROUP):
        by_group[q] = codes[pl.ds((q // 2) * 2 * NZ + q % 2, NZ, stride=2), :]

    loads[2].wait()
    loads[3].wait()
    relations = rel.shape[0]

    def table_step(i, carry):
        pair = jnp.concatenate([rel[2 * i], rel[2 * i + 1]], axis=1)
        got = jnp.dot(feat[...], pair, preferred_element_type=f32).astype(jnp.bfloat16)
        for b in range(BLOCKS):
            for h in range(2):
                table[b * relations + 2 * i + h] = got[b * BLK : (b + 1) * BLK, h * BLK : (h + 1) * BLK]
        return carry

    lax.fori_loop(0, relations // 2, table_step, 0, unroll=2)

    pl.semaphore_wait(barrier, GROUP - 1 + NZ - 1 + NY - 1)

    def group_copy(j):
        q = (p + j) % GROUP
        return pltpu.make_async_remote_copy(
            src_ref=by_group.at[q],
            dst_ref=group_got.at[pl.ds(pl.multiple_of(p * NZ, NZ), NZ)],
            send_sem=send1.at[j - 1],
            recv_sem=recv1.at[j - 1],
            device_id=at(dp_index(q // 2, z, q % 2)),
            device_id_type=MESH,
        )

    for j in range(1, GROUP):
        group_copy(j).start()
    group_got[pl.ds(pl.multiple_of(p * NZ, NZ), NZ), :] = by_group[p]

    def message_step(chunk, carry):
        adj_load(chunk).wait()
        per = PEERS // ADJ_CHUNKS
        step = 4

        def inner(i, carry):
            for u in range(step):
                d = chunk * per + i * step + u
                for k in range(SLOTS):
                    row = source_in[k, d] * relations + type_in[k, d]
                    n = d * SLOTS + k
                    msg[n] = jnp.dot(adj[n], table[row], preferred_element_type=f32)
            return carry

        return lax.fori_loop(0, per // step, inner, carry)

    lax.fori_loop(0, 4, message_step, 0)

    for j in range(1, GROUP):
        group_copy(j).wait_recv()
    for zi in range(NZ):
        by_z[zi] = group_got[pl.ds(zi, GROUP, stride=NZ), :]

    def z_copy(j):
        zi = (z + j) % NZ
        return pltpu.make_async_remote_copy(
            src_ref=by_z.at[zi],
            dst_ref=z_got.at[pl.ds(pl.multiple_of(z * GROUP, GROUP), GROUP)],
            send_sem=send2.at[j - 1],
            recv_sem=recv2.at[j - 1],
            device_id=at(dp_index(x, zi, c)),
            device_id_type=MESH,
        )

    for j in range(1, NZ):
        z_copy(j).start()
    z_got[pl.ds(pl.multiple_of(z * GROUP, GROUP), GROUP), :] = by_z[z]

    lax.fori_loop(4, ADJ_CHUNKS, message_step, 0)

    for load in loads[4:]:
        load.wait()
    base[...] = jnp.dot(feat[...], self_w[...], preferred_element_type=f32) + bias[...].astype(f32)

    for j in range(1, NZ):
        z_copy(j).wait_recv()
    routed = z_got[...]
    for k in range(SLOTS):
        column = jnp.broadcast_to(routed[:, k : k + 1], routed.shape)
        for b in range(BLOCKS):
            weight[k * BLOCKS + b] = (column == b).astype(f32)

    def own_sum(dx, dz, ci, b):
        xi = (x + dx) % NX
        zi = (z + dz) % NZ
        d = dp_index(xi, zi, ci)
        r = zi * GROUP + xi * 2 + ci
        total = None
        for k in range(SLOTS):
            term = msg[d * SLOTS + k] * weight[k * BLOCKS + b, pl.ds(r, 1), :]
            total = term if total is None else total + term
        return total

    other = 1 - c

    def core_copy(dz):
        return pltpu.make_async_remote_copy(
            src_ref=core_send.at[dz],
            dst_ref=core_got.at[dz],
            send_sem=core_s.at[dz],
            recv_sem=core_r.at[dz],
            device_id=at(dp_index(x, z, other)),
            device_id_type=MESH,
        )

    for dz in ROW_ORDER:

        def one(dx, carry, dz=dz):
            for b in range(BLOCKS):
                core_send[dz, dx, b] = own_sum(dx, dz, other, b).astype(jnp.bfloat16)
            return carry

        lax.fori_loop(0, NX, one, 0)
        core_copy(dz).start()

    def piece_copy(name):
        way = PIECES[name][4]
        to = {
            "x+": dp_index((x + 1) % NX, z, c),
            "x-": dp_index((x + NX - 1) % NX, z, c),
            "z+": dp_index(x, (z + 1) % NZ, c),
            "z-": dp_index(x, (z + NZ - 1) % NZ, c),
        }[way]
        n = SLOT_OF[name]
        return pltpu.make_async_remote_copy(
            src_ref=send_buf.at[n],
            dst_ref=got_buf.at[n],
            send_sem=piece_s.at[n],
            recv_sem=piece_r.at[n],
            device_id=at(to),
            device_id_type=MESH,
        )

    rows_in = set()
    pieces_in = set()
    for name in ORDER:
        dx, dz, b, adds, way = PIECES[name]
        if dz not in rows_in:
            core_copy(dz).wait_recv()
            rows_in.add(dz)
        for add in adds:
            if add not in pieces_in:
                piece_copy(add).wait_recv()
                pieces_in.add(add)
        total = own_sum(dx, dz, c, b) + core_got[dz, dx, b].astype(f32)
        for add in adds:
            total = total + got_buf[SLOT_OF[add]].astype(f32)
        if way is None:
            block = slice(b * BLK, (b + 1) * BLK)
            hidden[block, :] = jnp.maximum(base[block, :] + total, 0.0).astype(jnp.bfloat16)
        else:
            send_buf[SLOT_OF[name]] = total.astype(jnp.bfloat16)
            piece_copy(name).start()

    share = gathered.shape[1]

    def mp_copy(j):
        to = (y + j) % NY
        return pltpu.make_async_remote_copy(
            src_ref=hidden.at[pl.ds(pl.multiple_of(to * share, share), share)],
            dst_ref=gathered.at[y],
            send_sem=mp_s.at[j - 1],
            recv_sem=mp_r.at[j - 1],
            device_id=at(me, to),
            device_id_type=MESH,
        )

    for j in range(1, NY):
        mp_copy(j).start()
    gathered[y] = hidden[pl.ds(pl.multiple_of(y * share, share), share), :]
    for j in range(1, GROUP):
        group_copy(j).wait_send()
    for j in range(1, NZ):
        z_copy(j).wait_send()
    for dz in ROW_ORDER:
        core_copy(dz).wait_send()
    for name in SENT:
        piece_copy(name).wait_send()
    for j in range(1, NY):
        mp_copy(j).wait_recv()
    values = [gathered[i].astype(f32) for i in range(NY)]
    squares = sum(jnp.sum(v * v, axis=1, keepdims=True) for v in values)
    inverse = lax.rsqrt(squares / (NY * BLK) + EPSILON)
    for i, v in enumerate(values):
        cut = slice(i * BLK, (i + 1) * BLK)
        out_ref[:, cut] = (v * inverse * gain[i : i + 1, :].astype(f32)).astype(jnp.bfloat16)
    for j in range(1, NY):
        mp_copy(j).wait_send()


def per_device(
    features, adjacency, source_block, edge_type, target_block, live_count,
    relation_weight, self_weight, layer_bias, norm_gain,
):
    bf16, f32, i32 = jnp.bfloat16, jnp.float32, jnp.int32
    rows, width = features.shape
    relations = relation_weight.shape[0]
    slots = PEERS * SLOTS
    share = rows // NY
    dma = pltpu.SemaphoreType.DMA
    any_spec = pl.BlockSpec(memory_space=pl.ANY)
    smem_spec = pl.BlockSpec(memory_space=pltpu.SMEM)
    return pl.pallas_call(
        layer_kernel,
        name="layer",
        out_shape=jax.ShapeDtypeStruct((share, width), bf16),
        in_specs=[any_spec, any_spec, smem_spec, smem_spec] + [any_spec] * 6,
        out_specs=pl.BlockSpec(memory_space=pltpu.VMEM),
        scratch_shapes=[
            pltpu.VMEM((rows, width), bf16),
            pltpu.VMEM((slots, BLK, BLK), bf16),
            pltpu.VMEM((SLOTS, PEERS), i32),
            pltpu.VMEM((1, PEERS), i32),
            pltpu.VMEM((relations, width, BLK), bf16),
            pltpu.VMEM((width, BLK), bf16),
            pltpu.VMEM((1, BLK), bf16),
            pltpu.VMEM((NY, BLK), bf16),
            pltpu.VMEM((BLOCKS * relations, BLK, BLK), bf16),
            pltpu.VMEM((slots, BLK, BLK), f32),
            pltpu.VMEM((BLK, BLK), i32),
            pltpu.VMEM((GROUP, NZ, BLK), i32),
            pltpu.VMEM((PEERS, BLK), i32),
            pltpu.VMEM((NZ, GROUP, BLK), i32),
            pltpu.VMEM((PEERS, BLK), i32),
            pltpu.VMEM((SLOTS * BLOCKS, PEERS, BLK), f32),
            pltpu.VMEM((rows, BLK), f32),
            pltpu.VMEM((NZ, NX, BLOCKS, BLK, BLK), bf16),
            pltpu.VMEM((NZ, NX, BLOCKS, BLK, BLK), bf16),
            pltpu.VMEM((len(SENT), BLK, BLK), bf16),
            pltpu.VMEM((len(SENT), BLK, BLK), bf16),
            pltpu.VMEM((rows, BLK), bf16),
            pltpu.VMEM((NY, share, BLK), bf16),
            dma((7,)), dma((ADJ_CHUNKS,)),
            dma((GROUP - 1,)), dma((GROUP - 1,)), dma((NZ - 1,)), dma((NZ - 1,)),
            dma((NZ,)), dma((NZ,)), dma((len(SENT),)), dma((len(SENT),)), dma((NY - 1,)), dma((NY - 1,)),
        ],
        compiler_params=pltpu.CompilerParams(
            collective_id=0, has_side_effects=True, vmem_limit_bytes=60 * 1024 * 1024
        ),
    )(
        features, adjacency.reshape(slots, BLK, BLK), source_block.T, edge_type.T, target_block.T, live_count,
        relation_weight, self_weight, layer_bias.reshape(1, BLK), norm_gain.reshape(NY, BLK),
    )


def solution(mesh):
    return jax.shard_map(
        per_device,
        mesh=mesh,
        in_specs=(
            P("dp", None),
            P("dp", None, None, None),
            P("dp", None),
            P("dp", None),
            P("dp", None),
            P("dp", None),
            P(None, None, "mp"),
            P(None, "mp"),
            P("mp"),
            P(),
        ),
        out_specs=P(("dp", "mp"), None),
        check_vma=False,
    )
```

time: 230 us -> 52.6 us (0.23)
  the two profiles are of different devices: /device:TPU:1 before, /device:TPU:2 now
where the time goes in v1:
time: 52.6 us; the launch traced here: 52.4 us
  Pallas kernels  50.9 us (97%)
  local copies, waits for them, and re-layouts  1.47 us (3%)
    pallas_call x1, Pallas kernels, per_device(): pl.pallas_call(layer_kernel, name='layer', out_shape=jax.ShapeDtypeStruct...  50.9 us
    unnamed x1, local copies, waits for them, and re-layouts  1.47 us

profile of v1, /device:TPU:2, one launch (start us, length us, event | category | flops | bytes accessed | tf_op | source)
XLA Modules:
  0.0 52.4 jit_solution(5644959734343208626)
XLA Ops:
  0.0 50.9 %layer.1 = bf16[64,512]{1,0:T(8,128)(2,1)} custom-call(bf16[256,512]{1,0:T(8,128)(2,1)} %feat_in.1, bf16[256,128,128]{2,1,0:T(8,128)(2,1)} %bitcast.6, s32[4,64]{1,0:T(4,128)} %bitcast.7, s32[4,64]{1,0:T(4,128)} %bitcast.8, s32[4,64]{1,0:T(4,128)} %bitcast.9, s32[1,64]{1,0:T(1,128)} %live_in.1, bf16[20,512,128]{2,1,0:T(8,128)(2,1)} %rel_in.1, ...), custom_call_target="tpu_custom_call" | custom-call | tf_op jit(solution)/shard_map/layer/pallas_call | solution.py:331
  50.9 1.5 %copy.12 = bf16[64,512]{1,0:T(8,128)(2,1)} copy(bf16[64,512]{1,0:T(8,128)(2,1)} %layer.1) | data formatting | bytes 131072
